TPU v7x, 512 devices: a whole 4x8x8 slice. The times are simulated.
512 devices in a mesh: frame: 32 (over y_lo, z, core), space: 16 (over x, y_hi).
Axes of the slice: x: 4, y: 8 (y_hi: 4, y_lo: 2; y = y_hi * 2 + y_lo), z: 8, core: 2. Of those that a mesh axis runs over, the one named last changes fastest.
Arguments:
- spatial_query: bfloat16 [32, 1024, 1152], P('frame', 'space'), may hold values from -24 to 24
- spatial_key: bfloat16 [32, 1024, 1152], P('frame', 'space'), may hold values from -24 to 24
- spatial_value: bfloat16 [32, 1024, 1152], P('frame', 'space'), may hold values from -6 to 6
- latents: bfloat16 [32, 1024, 1152], P('frame', 'space'), may hold values from -6 to 6
- proj_weight: bfloat16 [1152, 1152], P('frame'), may hold values from -0.1875 to 0.1875
- proj_bias: float32 [1152], replicated, may hold values from -3 to 3
- residual_gate: float32 [1152], replicated, may hold values from 0.5 to 1.5
- temporal_shift: float32 [1152], replicated, may hold values from -3 to 3
- temporal_scale: float32 [1152], replicated, may hold values from -0.5 to 0.5
- temporal_weight: bfloat16 [1152, 3456], P('frame'), may hold values from -0.75 to 0.75
- clip_lengths: int32 [16], replicated, may hold values from 1 to 4, 32 in all
Outputs:
- hidden: float32 [32, 1024, 1152], P('frame', 'space')
- temporal_out: float32 [32, 1024, 1152], P('frame', 'space')
Inputs may be any that keep to these rules, and one draw needn't show every extreme that they name: `clip_lengths`: 16 clips fill the 32 frames in order; one clip has exactly 4 frames.
All inputs are finite; a program needn't handle non-finite values.
Results may differ from a plain program's by a relative error of at most 0.012.
Values may be sent and summed in bfloat16 or wider, within the bound.
A program may use at most 64 MiB of HBM per device.

v0:
```python
import math
import jax
import jax.numpy as jnp
from jax import lax
from jax.sharding import Mesh
from jax.sharding import PartitionSpec as P

HEADS = 16
FRAME = ("frame_0", "frame_1", "frame_2")
neg_fill = -1e30


def in_blocks(shard, dim, devices):
    before, after = (shard.shape[:dim], shard.shape[dim + 1 :])
    return jnp.moveaxis(shard.reshape(*before, devices, -1, *after), dim, 0)


def in_order(blocks, dim):
    shape = list(blocks.shape[1:])
    shape[dim] *= blocks.shape[0]
    return jnp.moveaxis(blocks, 0, dim).reshape(shape)


def exchange_in_order(blocks, axes, sequence):
    shape = [lax.axis_size(a) for a in axes]
    blocks = blocks.reshape(*shape, *blocks.shape[1:])
    for k in sequence:
        blocks = lax.all_to_all(blocks, axes[k], split_axis=k, concat_axis=k, tiled=True)
    return blocks.reshape(-1, *blocks.shape[len(axes) :])


def exchange_by_chip(shard, groups, sequence, split_dim, concat_dim):
    devices = lax.axis_size(groups[0]) * lax.axis_size(groups[1])
    blocks = in_blocks(shard, split_dim, devices)
    return in_order(exchange_in_order(blocks, groups, sequence), concat_dim)


def head_scores(query, keys):
    factor = 1.0 / math.sqrt(query.shape[-1])
    return jnp.einsum("fahd,fbhd->fhab", query, keys, preferred_element_type=jnp.float32) * factor


def frame_attention(parts):
    query, keys, values = parts
    frames, count, heads, head_dim = query.shape
    block = math.gcd(count, 512)
    blocks = jnp.moveaxis(query.reshape(frames, count // block, block, heads, head_dim), 1, 0)

    def one_block(rows):
        scores = head_scores(rows, keys)
        top = jnp.max(scores, axis=-1, keepdims=True)
        probs = jnp.exp(scores - top)
        total = jnp.sum(probs, axis=-1)
        mixed = jnp.einsum(
            "fhab,fbhd->fahd",
            probs.astype(jnp.bfloat16),
            values,
            preferred_element_type=jnp.float32,
        )
        return (mixed / jnp.transpose(total, (0, 2, 1))[..., None]).astype(jnp.bfloat16)

    result = lax.map(one_block, blocks)
    return jnp.moveaxis(result, 0, 1).reshape(frames, count, heads, head_dim)


def temporal_mix(packed, allowed):
    frames, count = (packed.shape[0], packed.shape[1])
    width = packed.shape[2] // 3
    head_dim = width // HEADS
    split = (frames, count, HEADS, head_dim)
    query = packed[:, :, :width].reshape(split)
    keys = packed[:, :, width : 2 * width].reshape(split)
    values = packed[:, :, 2 * width :].reshape(split)
    scores = jnp.einsum("anhd,bnhd->nhab", query, keys, preferred_element_type=jnp.float32) * (
        1.0 / math.sqrt(head_dim)
    )
    scores = jnp.where(allowed, scores, neg_fill)
    top = jnp.max(scores, axis=-1, keepdims=True)
    probs = jnp.exp(scores - top)
    total = jnp.sum(probs, axis=-1)
    mixed = jnp.einsum(
        "nhab,bnhd->anhd", probs.astype(jnp.bfloat16), values, preferred_element_type=jnp.float32
    )
    mixed = mixed / jnp.transpose(total, (2, 0, 1))[..., None]
    return mixed.reshape(frames, count, width)


def shards(
    spatial_query,
    spatial_key,
    spatial_value,
    latents,
    proj_weight,
    proj_bias,
    residual_gate,
    temporal_shift,
    temporal_scale,
    temporal_weight,
    clip_lengths,
):
    frames_dev, patches_dev, width = latents.shape
    head_dim = width // HEADS
    split = (frames_dev, patches_dev, HEADS, head_dim)
    query = spatial_query.reshape(split)
    mixed_heads = frame_attention(
        (
            lax.all_to_all(query, "space", split_axis=2, concat_axis=1, tiled=True),
            lax.all_to_all(
                spatial_key.reshape(split), "space", split_axis=2, concat_axis=1, tiled=True
            ),
            lax.all_to_all(
                spatial_value.reshape(split), "space", split_axis=2, concat_axis=1, tiled=True
            ),
        )
    )
    attended = lax.all_to_all(mixed_heads, "space", split_axis=1, concat_axis=2, tiled=True)
    rows = frames_dev * patches_dev
    flat = attended.reshape(rows, width)
    projected = jnp.dot(
        flat,
        lax.all_gather(proj_weight, FRAME, axis=0, tiled=True),
        preferred_element_type=jnp.float32,
    )
    hidden = latents.reshape(rows, width).astype(jnp.float32) + residual_gate * (
        projected + proj_bias
    )
    mean = jnp.mean(hidden, axis=-1, keepdims=True)
    centred = hidden - mean
    variance = jnp.mean(centred * centred, axis=-1, keepdims=True)
    normed = (
        centred * lax.rsqrt(variance + 1e-06) * (1.0 + temporal_scale) + temporal_shift
    ).astype(jnp.bfloat16)
    groups = lax.axis_size(FRAME)
    frames_all = frames_dev * groups
    per_group = patches_dev // groups
    ends = jnp.cumsum(clip_lengths)
    clip_of = jnp.sum(
        (jnp.arange(frames_all, dtype=jnp.int32)[:, None] >= ends[None, :]).astype(jnp.int32),
        axis=1,
    )
    allowed = clip_of[:, None] == clip_of[None, :]
    whole_weight = lax.all_gather(temporal_weight, FRAME, axis=0, tiled=True)
    local = jnp.einsum(
        "fnc,ce->fne",
        exchange_by_chip(
            normed.reshape(frames_dev, groups, per_group, width),
            (("frame_0", "frame_1"), "frame_2"),
            (1, 0),
            1,
            0,
        )[:, 0],
        whole_weight,
        preferred_element_type=jnp.float32,
    ).astype(jnp.bfloat16)
    temporal = temporal_mix(local, allowed)[:, None]
    temporal = temporal.reshape(frames_all, per_group, width)
    temporal_out = lax.all_to_all(
        temporal.astype(jnp.bfloat16), FRAME, split_axis=0, concat_axis=1, tiled=True
    ).astype(temporal.dtype)
    return (hidden.reshape(frames_dev, patches_dev, width), temporal_out)


def solution(mesh):
    split = Mesh(
        mesh.devices.reshape(2, 8, 2, mesh.shape["space"]),
        ("frame_0", "frame_1", "frame_2", "space"),
    )
    return jax.shard_map(
        shards,
        mesh=split,
        in_specs=(
            P(FRAME, "space", None),
            P(FRAME, "space", None),
            P(FRAME, "space", None),
            P(FRAME, "space", None),
            P(FRAME, None),
            P(),
            P(),
            P(),
            P(),
            P(FRAME, None),
            P(),
        ),
        out_specs=(P(FRAME, "space", None), P(FRAME, "space", None)),
        check_vma=False,
    )
```

profile of v0, /device:TPU:1, one launch (start us, length us, event | category | flops | bytes accessed | tf_op | source)
XLA Modules:
  0.0 205.7 jit_solution(14141695110795643575)
XLA Ops:
  8.7 1.4 reshape.123
  10.0 0.8 copy.88
  10.8 10.2 %all-to-all-start = ((bf16[1,64,16,72]{3,1,0,2:T(8,128)(2,1)}), bf16[1,64,16,72]{3,1,0,2:T(8,128)(2,1)S(1)}, u32[]{:S(2)}, u32[]{:S(2)}) async-start(bf16[1,64,16,72]{3,1,0,2:T(8,128)(2,1)} %copy.88), calls=%async_computation | async-start | bytes 524288 | tf_op jit(solution)/shard_map/all_to_all | solution.py:107
  21.0 1.4 reshape.124
  22.4 0.8 copy.90
  23.2 10.2 %all-to-all-done = bf16[1,64,16,72]{3,1,0,2:T(8,128)(2,1)S(1)} async-done(((bf16[1,64,16,72]{3,1,0,2:T(8,128)(2,1)}), bf16[1,64,16,72]{3,1,0,2:T(8,128)(2,1)S(1)}, u32[]{:S(2)}, u32[]{:S(2)}) %all-to-all-start) | async-done | bytes 147488 | tf_op jit(solution)/shard_map/all_to_all | solution.py:107
  33.4 3.9 %all-to-all-start.1 = ((bf16[1,64,16,72]{3,1,0,2:T(8,128)(2,1)}), bf16[1,64,16,72]{3,1,0,2:T(8,128)(2,1)S(1)}, u32[]{:S(2)}, u32[]{:S(2)}) async-start(bf16[1,64,16,72]{3,1,0,2:T(8,128)(2,1)} %copy.90), calls=%async_computation.1 | async-start | bytes 524288 | tf_op jit(solution)/shard_map/all_to_all | solution.py:108
  37.7 0.8 copy.92
  38.5 13.1 %all-to-all-done.1 = bf16[1,64,16,72]{3,1,0,2:T(8,128)(2,1)S(1)} async-done(((bf16[1,64,16,72]{3,1,0,2:T(8,128)(2,1)}), bf16[1,64,16,72]{3,1,0,2:T(8,128)(2,1)S(1)}, u32[]{:S(2)}, u32[]{:S(2)}) %all-to-all-start.1) | async-done | bytes 147488 | tf_op jit(solution)/shard_map/all_to_all | solution.py:108
  51.6 3.5 %all-to-all-start.2 = ((bf16[1,64,16,72]{3,1,0,2:T(8,128)(2,1)}), bf16[1,64,16,72]{3,1,0,2:T(8,128)(2,1)S(1)}, u32[]{:S(2)}, u32[]{:S(2)}) async-start(bf16[1,64,16,72]{3,1,0,2:T(8,128)(2,1)} %copy.92), calls=%async_computation.2 | async-start | bytes 524288 | tf_op jit(solution)/shard_map/all_to_all | solution.py:111
  55.4 14.1 %all-to-all-done.2 = bf16[1,64,16,72]{3,1,0,2:T(8,128)(2,1)S(1)} async-done(((bf16[1,64,16,72]{3,1,0,2:T(8,128)(2,1)}), bf16[1,64,16,72]{3,1,0,2:T(8,128)(2,1)S(1)}, u32[]{:S(2)}, u32[]{:S(2)}) %all-to-all-start.2) | async-done | bytes 147488 | tf_op jit(solution)/shard_map/all_to_all | solution.py:111
  69.7 3.4 %while.10 = (s32[]{:T(128)}, bf16[2,1,512,1,72]{2,4,3,1,0:T(8,128)(2,1)S(1)}, bf16[2,1,512,1,72]{2,4,3,1,0:T(8,128)(2,1)S(1)}, bf16[1,1024,1,72]{1,3,2,0:T(8,128...) while((s32[]{:T(128)}, bf16[2,1,512,1,72]{2,4,3,1,0:T(8,128)(2,1)S(1)}, ...), condition=%wide.region_3.4_spmd, body=%wide.region_0.3_spmd.sunk | while | flops 155261952 | bytes 6744149 | solution.py:62
  73.9 2.3 %reduce.5 = bf16[1024,72]{1,0:T(8,128)(2,1)S(1)} reduce(bf16[1024,1,1,72]{3,2,1,0:T(2,128)(2,1)S(1)} %bitcast.98, bf16[]{:T(256)} %broadcast.46), dimensions={1,2}, to_apply=%bitcast.78.reduce_sub_computation | reduce | bytes 294914
  76.2 1.2 reshape.144
  77.4 3.5 %all-to-all-start.3 = ((bf16[16,2,2304]{2,1,0:T(2,128)(2,1)}), bf16[16,2,2304]{2,1,0:T(2,128)(2,1)S(1)}, u32[]{:S(2)}, u32[]{:S(2)}) async-start(bf16[16,2,2304]{2,1,0:T(2,128)(2,1)} %reshape.144), calls=%async_computation.3 | async-start | bytes 294912 | tf_op jit(solution)/shard_map/all_to_all | solution.py:116
  81.2 9.5 %all-to-all-done.3 = bf16[16,2,2304]{2,1,0:T(2,128)(2,1)S(1)} async-done(((bf16[16,2,2304]{2,1,0:T(2,128)(2,1)}), bf16[16,2,2304]{2,1,0:T(2,128)(2,1)S(1)}, u32[]{:S(2)}, u32[]{:S(2)}) %all-to-all-start.3) | async-done | bytes 147488 | tf_op jit(solution)/shard_map/all_to_all | solution.py:116
  90.7 0.9 reshape.145
  92.9 3.6 %reshape.136 = bf16[1152,1152]{1,0:T(8,128)(2,1)S(1)} reshape(bf16[32,36,1152]{2,1,0:T(8,128)(2,1)} %all-gather.5.cloned.1.call-done) | data formatting | bytes 5308416
  97.8 6.7 %all_to_all.85 = bf16[16,2,1,1,2,1152]{5,4,0,3,2,1:T(2,128)(2,1)S(1)} all-to-all(bf16[16,2,1,1,2,1152]{5,4,0,3,2,1:T(2,128)(2,1)S(1)} %copy.99), channel_id=1, replica_groups=mesh['frame_0'=2,'frame_1'=8,'frame_2'=2,'space'=16] {'frame_2'}, dimensions={1} | all-to-all | bytes 294912 | tf_op jit(solution)/shard_map/all_to_all | solution.py:28
  105.3 9.1 %all-to-all-start.5 = ((bf16[16,2,1,1,2,1152]{5,4,1,3,2,0:T(2,128)(2,1)}), bf16[16,2,1,1,2,1152]{5,4,1,3,2,0:T(2,128)(2,1)S(1)}, u32[]{:S(2)}, u32[]{:S(2)}) async-start(bf16[16,2,1,1,2,1152]{5,4,1,3,2,0:T(2,128)(2,1)} %copy.100), calls=%async_computation.5 | async-start | bytes 294912 | tf_op jit(solution)/shard_map/all_to_all | solution.py:28
  114.6 49.2 %all-gather.7.cloned.1.call-done = bf16[32,36,3456]{2,1,0:T(8,128)(2,1)} async-done(((bf16[1,36,3456]{2,1,0:T(8,128)(2,1)}), bf16[32,36,3456]{2,1,0:T(8,128)(2,1)}) %all-gather.7.cloned.1.call-update) | async-done | bytes 7962640 | tf_op jit(solution)/shard_map/all_gather | solution.py:142
  163.8 12.4 %reshape.139 = bf16[1152,3456,1]{1,0,2:T(8,128)(2,1)} reshape(bf16[32,36,3456]{2,1,0:T(8,128)(2,1)} %all-gather.7.cloned.1.call-done) | data formatting | bytes 15925248
  176.2 4.6 %convolution_convert_fusion = bf16[32,2,3456]{2,0,1:T(8,128)(2,1)S(1)} fusion(bf16[1152,3456,1]{1,0,2:T(8,128)(2,1)} %reshape.139, bf16[32,2,1152]{2,1,0:T(2,128)(2,1)S(1)} %bitcast.104), kind=kOutput, calls=%fused_computation.16 | convolution fusion | flops 509829120 | bytes 8552448 | tf_op jit(solution)/shard_map/fnc,ce->fne/dot_general | solution.py:143
  183.5 14.6 %all_to_all.86 = bf16[32,2,1152]{2,1,0:T(2,128)(2,1)S(1)} all-to-all(bf16[32,2,1152]{2,1,0:T(2,128)(2,1)S(1)} %reshape.142), channel_id=1, replica_groups=mesh['frame_0'=2,'frame_1'=8,'frame_2'=2,'space'=16] {'frame_0','frame_1..., dimensions={0} | all-to-all | bytes 294912 | tf_op jit(solution)/shard_map/all_to_all | solution.py:157
  (64 shorter events, 13.5 us)
Async XLA Ops:
  7.2 30.1 %copy-start.1 = (bf16[1,64,1152]{2,1,0:T(8,128)(2,1)S(1)}, bf16[1,64,1152]{2,1,0:T(8,128)(2,1)}, u32[]{:S(2)}) copy-start(bf16[1,64,1152]{2,1,0:T(8,128)(2,1)} %param.15) | copy-start | bytes 442372
  7.2 85.7 %all-gather.5.cloned.1.call-start = ((), (), s32[]{:S(2)}) async-start(), calls=%async_computation.7 | async-start | bytes 3041280 | tf_op jit(solution)/shard_map/all_gather | solution.py:121
  7.9 155.8 %all-gather.7.cloned.1.call-start = ((), (), s32[]{:S(2)}) async-start(), calls=%async_computation.8 | async-start | bytes 9123840 | tf_op jit(solution)/shard_map/all_gather | solution.py:142
  10.8 22.6 %all-to-all-start = ((bf16[1,64,16,72]{3,1,0,2:T(8,128)(2,1)}), bf16[1,64,16,72]{3,1,0,2:T(8,128)(2,1)S(1)}, u32[]{:S(2)}, u32[]{:S(2)}) async-start(bf16[1,64,16,72]{3,1,0,2:T(8,128)(2,1)} %copy.88), calls=%async_computation | async-start | bytes 524288 | tf_op jit(solution)/shard_map/all_to_all | solution.py:107
  33.4 18.2 %all-to-all-start.1 = ((bf16[1,64,16,72]{3,1,0,2:T(8,128)(2,1)}), bf16[1,64,16,72]{3,1,0,2:T(8,128)(2,1)S(1)}, u32[]{:S(2)}, u32[]{:S(2)}) async-start(bf16[1,64,16,72]{3,1,0,2:T(8,128)(2,1)} %copy.90), calls=%async_computation.1 | async-start | bytes 524288 | tf_op jit(solution)/shard_map/all_to_all | solution.py:108
  51.6 18.0 %all-to-all-start.2 = ((bf16[1,64,16,72]{3,1,0,2:T(8,128)(2,1)}), bf16[1,64,16,72]{3,1,0,2:T(8,128)(2,1)S(1)}, u32[]{:S(2)}, u32[]{:S(2)}) async-start(bf16[1,64,16,72]{3,1,0,2:T(8,128)(2,1)} %copy.92), calls=%async_computation.2 | async-start | bytes 524288 | tf_op jit(solution)/shard_map/all_to_all | solution.py:111
  73.1 7.8 %copy-start.7 = (s32[16]{0:T(128)S(1)}, s32[16]{0:T(128)}, u32[]{:S(2)}) copy-start(s32[16]{0:T(128)} %param.23) | copy-start | bytes 196
  73.1 8.1 %copy-start.6 = (f32[1152]{0:T(1024)S(1)}, f32[1152]{0:T(1024)}, u32[]{:S(2)}) copy-start(f32[1152]{0:T(1024)} %param.21) | copy-start | bytes 13828
  77.4 13.3 %all-to-all-start.3 = ((bf16[16,2,2304]{2,1,0:T(2,128)(2,1)}), bf16[16,2,2304]{2,1,0:T(2,128)(2,1)S(1)}, u32[]{:S(2)}, u32[]{:S(2)}) async-start(bf16[16,2,2304]{2,1,0:T(2,128)(2,1)} %reshape.144), calls=%async_computation.3 | async-start | bytes 294912 | tf_op jit(solution)/shard_map/all_to_all | solution.py:116
  92.8 3.7 %copy-start.2 = (bf16[1,64,1152]{2,1,0:T(8,128)(2,1)S(1)}, bf16[1,64,1152]{2,1,0:T(8,128)(2,1)}, u32[]{:S(2)}) copy-start(bf16[1,64,1152]{2,1,0:T(8,128)(2,1)} %param.16) | copy-start | bytes 442372
  92.9 3.7 %copy-start.3 = (f32[1152]{0:T(1024)S(1)}, f32[1152]{0:T(1024)}, u32[]{:S(2)}) copy-start(f32[1152]{0:T(1024)} %param.18) | copy-start | bytes 13828
  92.9 3.7 %copy-start.4 = (f32[1152]{0:T(1024)S(1)}, f32[1152]{0:T(1024)}, u32[]{:S(2)}) copy-start(f32[1152]{0:T(1024)} %param.19) | copy-start | bytes 13828
  96.6 0.9 copy-start.5
  97.3 78.9 %copy-start = (f32[64,1152]{1,0:T(8,128)}, f32[64,1152]{1,0:T(8,128)S(1)}, u32[]{:S(2)}) copy-start(f32[64,1152]{1,0:T(8,128)S(1)} %get-tuple-element.71) | copy-start | bytes 884740
  105.3 70.9 %all-to-all-start.5 = ((bf16[16,2,1,1,2,1152]{5,4,1,3,2,0:T(2,128)(2,1)}), bf16[16,2,1,1,2,1152]{5,4,1,3,2,0:T(2,128)(2,1)S(1)}, u32[]{:S(2)}, u32[]{:S(2)}) async-start(bf16[16,2,1,1,2,1152]{5,4,1,3,2,0:T(2,128)(2,1)} %copy.100), calls=%async_computation.5 | async-start | bytes 294912 | tf_op jit(solution)/shard_map/all_to_all | solution.py:28
Sparse Core Ops, SparseCore 0:
  10.1 74.3 all-gather.4
  86.6 77.0 all-gather.6
where the time goes:
time: 207 us; the launch traced here: 206 us
  waiting for transfers between devices  97.6 us (47%)
  starting transfers between devices  30.3 us (15%)
  local copies, waits for them, and re-layouts  29.8 us (14%)
  blocking collectives  21.3 us (10%)
  between operations  14.4 us (7%)
  matrix products  8.13 us (4%)
  other arithmetic  4.11 us (2%)
    all_gather x1, waiting for transfers between devices, shards(): whole_weight = lax.all_gather(temporal_weight, FRAME, axis=0, tiled=True)  49.2 us
    unnamed x21, local copies, waits for them, and re-layouts  18.7 us
    all_to_all x1, blocking collectives, shards(): lax.all_to_all(temporal.astype(jnp.bfloat16), FRAME, split_axis=0, concat...  14.6 us
    all_to_all x1, waiting for transfers between devices, shards(): lax.all_to_all(spatial_value.reshape(split), 'space', split_axis=2, conca...  14.1 us
    all_to_all x1, waiting for transfers between devices, shards(): lax.all_to_all(spatial_key.reshape(split), 'space', split_axis=2, concat_...  13.1 us
    all_to_all x1, starting transfers between devices, shards(): lax.all_to_all(query, 'space', split_axis=2, concat_axis=1, tiled=True)  10.2 us
    all_to_all x1, waiting for transfers between devices, shards(): lax.all_to_all(query, 'space', split_axis=2, concat_axis=1, tiled=True)  10.2 us
    all_to_all x1, waiting for transfers between devices, shards(): lax.all_to_all(mixed_heads, 'space', split_axis=1, concat_axis=2, tiled=T...  9.53 us
  transfers between devices with their start and end apart: 7, of which 5 were waited for; matrix products, arithmetic and copies ran while one was open for 16% of the time, Pallas kernels for 0%

commit v1 on v0

--- a/solution.py
+++ b/solution.py
@@ -8,6 +8,15 @@
 HEADS = 16
 FRAME = ("frame_0", "frame_1", "frame_2")
 neg_fill = -1e30
+
+
+def begin_views(vec):
+    return jnp.concatenate(
+        jax.lax.all_to_all(
+            jnp.stack(jnp.split(vec, jax.lax.axis_size(FRAME), axis=0)), FRAME, 0, 0
+        ),
+        axis=1,
+    )
 
 
 def in_blocks(shard, dim, devices):
@@ -154,9 +163,7 @@
     ).astype(jnp.bfloat16)
     temporal = temporal_mix(local, allowed)[:, None]
     temporal = temporal.reshape(frames_all, per_group, width)
-    temporal_out = lax.all_to_all(
-        temporal.astype(jnp.bfloat16), FRAME, split_axis=0, concat_axis=1, tiled=True
-    ).astype(temporal.dtype)
+    temporal_out = begin_views(temporal.astype(jnp.bfloat16)).astype(temporal.dtype)
     return (hidden.reshape(frames_dev, patches_dev, width), temporal_out)
 
 

time: 207 us -> 212 us (1.024)
  local copies, waits for them, and re-layouts: 29.8 us -> 34.3 us
    another operation x1 -> x34, local copies, waits for them, and re-layouts: 0.08 us -> 3.16 us  [the longest x33 3.08 us: begin_views(): jnp.stack(jnp.split(vec, jax.lax.axis_size(FRAME), axis=0))]
    unnamed x21 -> x52, local copies, waits for them, and re-layouts: 18.7 us -> 19.1 us
where the time goes in v1:
time: 212 us; the launch traced here: 211 us
  waiting for transfers between devices  97.6 us (46%)
  local copies, waits for them, and re-layouts  34.3 us (16%)
  starting transfers between devices  30.3 us (14%)
  blocking collectives  21.3 us (10%)
  between operations  14.7 us (7%)
  matrix products  8.13 us (4%)
  other arithmetic  4.11 us (2%)
    all_gather x1, waiting for transfers between devices, shards(): whole_weight = lax.all_gather(temporal_weight, FRAME, axis=0, tiled=True)  49.2 us
    unnamed x52, local copies, waits for them, and re-layouts  19.1 us
    all_to_all x1, blocking collectives, begin_views(): jax.lax.all_to_all(jnp.stack(jnp.split(vec, jax.lax.axis_size(FRAME), axi...  14.6 us
    all_to_all x1, waiting for transfers between devices, shards(): lax.all_to_all(spatial_value.reshape(split), 'space', split_axis=2, conca...  14.1 us
    all_to_all x1, waiting for transfers between devices, shards(): lax.all_to_all(spatial_key.reshape(split), 'space', split_axis=2, concat_...  13.1 us
    all_to_all x1, starting transfers between devices, shards(): lax.all_to_all(query, 'space', split_axis=2, concat_axis=1, tiled=True)  10.2 us
    all_to_all x1, waiting for transfers between devices, shards(): lax.all_to_all(query, 'space', split_axis=2, concat_axis=1, tiled=True)  10.2 us
    all_to_all x1, waiting for transfers between devices, shards(): lax.all_to_all(mixed_heads, 'space', split_axis=1, concat_axis=2, tiled=T...  9.53 us
  transfers between devices with their start and end apart: 7, of which 5 were waited for; matrix products, arithmetic and copies ran while one was open for 16% of the time, Pallas kernels for 0%

profile of v1, /device:TPU:1, one launch (start us, length us, event | category | flops | bytes accessed | tf_op | source)
XLA Modules:
  0.0 210.5 jit_solution(3830157419786683748)
XLA Ops:
  8.7 1.4 reshape.185
  10.0 0.8 copy.69
  10.8 10.2 %all-to-all-start = ((bf16[1,64,16,72]{3,1,0,2:T(8,128)(2,1)}), bf16[1,64,16,72]{3,1,0,2:T(8,128)(2,1)S(1)}, u32[]{:S(2)}, u32[]{:S(2)}) async-start(bf16[1,64,16,72]{3,1,0,2:T(8,128)(2,1)} %copy.69), calls=%async_computation | async-start | bytes 524288 | tf_op jit(solution)/shard_map/all_to_all | solution.py:116
  21.0 1.4 reshape.186
  22.4 0.8 copy.71
  23.2 10.2 %all-to-all-done = bf16[1,64,16,72]{3,1,0,2:T(8,128)(2,1)S(1)} async-done(((bf16[1,64,16,72]{3,1,0,2:T(8,128)(2,1)}), bf16[1,64,16,72]{3,1,0,2:T(8,128)(2,1)S(1)}, u32[]{:S(2)}, u32[]{:S(2)}) %all-to-all-start) | async-done | bytes 147488 | tf_op jit(solution)/shard_map/all_to_all | solution.py:116
  33.4 3.9 %all-to-all-start.1 = ((bf16[1,64,16,72]{3,1,0,2:T(8,128)(2,1)}), bf16[1,64,16,72]{3,1,0,2:T(8,128)(2,1)S(1)}, u32[]{:S(2)}, u32[]{:S(2)}) async-start(bf16[1,64,16,72]{3,1,0,2:T(8,128)(2,1)} %copy.71), calls=%async_computation.1 | async-start | bytes 524288 | tf_op jit(solution)/shard_map/all_to_all | solution.py:117
  38.5 13.1 %all-to-all-done.1 = bf16[1,64,16,72]{3,1,0,2:T(8,128)(2,1)S(1)} async-done(((bf16[1,64,16,72]{3,1,0,2:T(8,128)(2,1)}), bf16[1,64,16,72]{3,1,0,2:T(8,128)(2,1)S(1)}, u32[]{:S(2)}, u32[]{:S(2)}) %all-to-all-start.1) | async-done | bytes 147488 | tf_op jit(solution)/shard_map/all_to_all | solution.py:117
  51.6 3.5 %all-to-all-start.2 = ((bf16[1,64,16,72]{3,1,0,2:T(8,128)(2,1)}), bf16[1,64,16,72]{3,1,0,2:T(8,128)(2,1)S(1)}, u32[]{:S(2)}, u32[]{:S(2)}) async-start(bf16[1,64,16,72]{3,1,0,2:T(8,128)(2,1)} %copy.73), calls=%async_computation.2 | async-start | bytes 524288 | tf_op jit(solution)/shard_map/all_to_all | solution.py:120
  55.4 14.1 %all-to-all-done.2 = bf16[1,64,16,72]{3,1,0,2:T(8,128)(2,1)S(1)} async-done(((bf16[1,64,16,72]{3,1,0,2:T(8,128)(2,1)}), bf16[1,64,16,72]{3,1,0,2:T(8,128)(2,1)S(1)}, u32[]{:S(2)}, u32[]{:S(2)}) %all-to-all-start.2) | async-done | bytes 147488 | tf_op jit(solution)/shard_map/all_to_all | solution.py:120
  69.7 3.4 %while.10 = (s32[]{:T(128)}, bf16[2,1,512,1,72]{2,4,3,1,0:T(8,128)(2,1)S(1)}, bf16[2,1,512,1,72]{2,4,3,1,0:T(8,128)(2,1)S(1)}, bf16[1,1024,1,72]{1,3,2,0:T(8,128...) while((s32[]{:T(128)}, bf16[2,1,512,1,72]{2,4,3,1,0:T(8,128)(2,1)S(1)}, ...), condition=%wide.region_3.4_spmd, body=%wide.region_0.3_spmd.sunk | while | flops 155261952 | bytes 6744149 | solution.py:71
  73.9 2.3 %reduce.69 = bf16[1024,72]{1,0:T(8,128)(2,1)S(1)} reduce(bf16[1024,1,1,72]{3,2,1,0:T(2,128)(2,1)S(1)} %bitcast.96, bf16[]{:T(256)} %broadcast.78), dimensions={1,2}, to_apply=%bitcast.76.reduce_sub_computation | reduce | bytes 294914
  76.2 1.2 reshape.237
  77.4 3.5 %all-to-all-start.3 = ((bf16[16,2,2304]{2,1,0:T(2,128)(2,1)}), bf16[16,2,2304]{2,1,0:T(2,128)(2,1)S(1)}, u32[]{:S(2)}, u32[]{:S(2)}) async-start(bf16[16,2,2304]{2,1,0:T(2,128)(2,1)} %reshape.237), calls=%async_computation.3 | async-start | bytes 294912 | tf_op jit(solution)/shard_map/all_to_all | solution.py:125
  81.2 9.5 %all-to-all-done.3 = bf16[16,2,2304]{2,1,0:T(2,128)(2,1)S(1)} async-done(((bf16[16,2,2304]{2,1,0:T(2,128)(2,1)}), bf16[16,2,2304]{2,1,0:T(2,128)(2,1)S(1)}, u32[]{:S(2)}, u32[]{:S(2)}) %all-to-all-start.3) | async-done | bytes 147488 | tf_op jit(solution)/shard_map/all_to_all | solution.py:125
  90.7 0.9 reshape.238
  92.9 3.6 %reshape.198 = bf16[1152,1152]{1,0:T(8,128)(2,1)S(1)} reshape(bf16[32,36,1152]{2,1,0:T(8,128)(2,1)} %all-gather.5.cloned.1.call-done) | data formatting | bytes 5308416
  97.8 6.7 %all_to_all.81 = bf16[16,2,1,1,2,1152]{5,4,0,3,2,1:T(2,128)(2,1)S(1)} all-to-all(bf16[16,2,1,1,2,1152]{5,4,0,3,2,1:T(2,128)(2,1)S(1)} %copy.80), channel_id=1, replica_groups=mesh['frame_0'=2,'frame_1'=8,'frame_2'=2,'space'=16] {'frame_2'}, dimensions={1} | all-to-all | bytes 294912 | tf_op jit(solution)/shard_map/all_to_all | solution.py:37
  105.3 9.1 %all-to-all-start.5 = ((bf16[16,2,1,1,2,1152]{5,4,1,3,2,0:T(2,128)(2,1)}), bf16[16,2,1,1,2,1152]{5,4,1,3,2,0:T(2,128)(2,1)S(1)}, u32[]{:S(2)}, u32[]{:S(2)}) async-start(bf16[16,2,1,1,2,1152]{5,4,1,3,2,0:T(2,128)(2,1)} %copy.81), calls=%async_computation.5 | async-start | bytes 294912 | tf_op jit(solution)/shard_map/all_to_all | solution.py:37
  114.6 49.2 %all-gather.7.cloned.1.call-done = bf16[32,36,3456]{2,1,0:T(8,128)(2,1)} async-done(((bf16[1,36,3456]{2,1,0:T(8,128)(2,1)}), bf16[32,36,3456]{2,1,0:T(8,128)(2,1)}) %all-gather.7.cloned.1.call-update) | async-done | bytes 7962640 | tf_op jit(solution)/shard_map/all_gather | solution.py:151
  163.8 12.4 %reshape.201 = bf16[1152,3456,1]{1,0,2:T(8,128)(2,1)} reshape(bf16[32,36,3456]{2,1,0:T(8,128)(2,1)} %all-gather.7.cloned.1.call-done) | data formatting | bytes 15925248
  176.2 4.6 %convolution_convert_fusion = bf16[32,2,3456]{2,0,1:T(8,128)(2,1)S(1)} fusion(bf16[1152,3456,1]{1,0,2:T(8,128)(2,1)} %reshape.201, bf16[32,2,1152]{2,1,0:T(2,128)(2,1)S(1)} %bitcast.102), kind=kOutput, calls=%fused_computation.16 | convolution fusion | flops 509829120 | bytes 8552448 | tf_op jit(solution)/shard_map/fnc,ce->fne/dot_general | solution.py:152
  183.6 0.9 slice_reduce_fusion
  188.3 14.6 %all_to_all.82 = bf16[32,1,2,1152]{3,2,1,0:T(2,128)(2,1)S(1)} all-to-all(bf16[32,1,2,1152]{3,2,1,0:T(2,128)(2,1)S(1)} %constant_dynamic-update-slice_fusion), channel_id=1, replica_groups=mesh['frame_0'=2,'frame_1'=8,'frame_2'=2,'space'=16] {'frame_0','frame_1..., dimensions={0} | all-to-all | bytes 294912 | tf_op jit(solution)/shard_map/all_to_all | solution.py:15
  (128 shorter events, 17.9 us)
Async XLA Ops:
  7.2 30.1 %copy-start.1 = (bf16[1,64,1152]{2,1,0:T(8,128)(2,1)S(1)}, bf16[1,64,1152]{2,1,0:T(8,128)(2,1)}, u32[]{:S(2)}) copy-start(bf16[1,64,1152]{2,1,0:T(8,128)(2,1)} %param.15) | copy-start | bytes 442372
  7.2 85.7 %all-gather.5.cloned.1.call-start = ((), (), s32[]{:S(2)}) async-start(), calls=%async_computation.7 | async-start | bytes 3041280 | tf_op jit(solution)/shard_map/all_gather | solution.py:130
  7.9 155.8 %all-gather.7.cloned.1.call-start = ((), (), s32[]{:S(2)}) async-start(), calls=%async_computation.8 | async-start | bytes 9123840 | tf_op jit(solution)/shard_map/all_gather | solution.py:151
  10.8 22.6 %all-to-all-start = ((bf16[1,64,16,72]{3,1,0,2:T(8,128)(2,1)}), bf16[1,64,16,72]{3,1,0,2:T(8,128)(2,1)S(1)}, u32[]{:S(2)}, u32[]{:S(2)}) async-start(bf16[1,64,16,72]{3,1,0,2:T(8,128)(2,1)} %copy.69), calls=%async_computation | async-start | bytes 524288 | tf_op jit(solution)/shard_map/all_to_all | solution.py:116
  33.4 18.2 %all-to-all-start.1 = ((bf16[1,64,16,72]{3,1,0,2:T(8,128)(2,1)}), bf16[1,64,16,72]{3,1,0,2:T(8,128)(2,1)S(1)}, u32[]{:S(2)}, u32[]{:S(2)}) async-start(bf16[1,64,16,72]{3,1,0,2:T(8,128)(2,1)} %copy.71), calls=%async_computation.1 | async-start | bytes 524288 | tf_op jit(solution)/shard_map/all_to_all | solution.py:117
  51.6 18.0 %all-to-all-start.2 = ((bf16[1,64,16,72]{3,1,0,2:T(8,128)(2,1)}), bf16[1,64,16,72]{3,1,0,2:T(8,128)(2,1)S(1)}, u32[]{:S(2)}, u32[]{:S(2)}) async-start(bf16[1,64,16,72]{3,1,0,2:T(8,128)(2,1)} %copy.73), calls=%async_computation.2 | async-start | bytes 524288 | tf_op jit(solution)/shard_map/all_to_all | solution.py:120
  73.1 7.8 %copy-start.7 = (s32[16]{0:T(128)S(1)}, s32[16]{0:T(128)}, u32[]{:S(2)}) copy-start(s32[16]{0:T(128)} %param.23) | copy-start | bytes 196
  73.1 8.1 %copy-start.6 = (f32[1152]{0:T(1024)S(1)}, f32[1152]{0:T(1024)}, u32[]{:S(2)}) copy-start(f32[1152]{0:T(1024)} %param.21) | copy-start | bytes 13828
  77.4 13.3 %all-to-all-start.3 = ((bf16[16,2,2304]{2,1,0:T(2,128)(2,1)}), bf16[16,2,2304]{2,1,0:T(2,128)(2,1)S(1)}, u32[]{:S(2)}, u32[]{:S(2)}) async-start(bf16[16,2,2304]{2,1,0:T(2,128)(2,1)} %reshape.237), calls=%async_computation.3 | async-start | bytes 294912 | tf_op jit(solution)/shard_map/all_to_all | solution.py:125
  92.8 3.7 %copy-start.2 = (bf16[1,64,1152]{2,1,0:T(8,128)(2,1)S(1)}, bf16[1,64,1152]{2,1,0:T(8,128)(2,1)}, u32[]{:S(2)}) copy-start(bf16[1,64,1152]{2,1,0:T(8,128)(2,1)} %param.16) | copy-start | bytes 442372
  92.9 3.7 %copy-start.3 = (f32[1152]{0:T(1024)S(1)}, f32[1152]{0:T(1024)}, u32[]{:S(2)}) copy-start(f32[1152]{0:T(1024)} %param.18) | copy-start | bytes 13828
  92.9 3.7 %copy-start.4 = (f32[1152]{0:T(1024)S(1)}, f32[1152]{0:T(1024)}, u32[]{:S(2)}) copy-start(f32[1152]{0:T(1024)} %param.19) | copy-start | bytes 13828
  96.6 0.9 copy-start.5
  97.3 78.9 %copy-start = (f32[64,1152]{1,0:T(8,128)}, f32[64,1152]{1,0:T(8,128)S(1)}, u32[]{:S(2)}) copy-start(f32[64,1152]{1,0:T(8,128)S(1)} %get-tuple-element.98) | copy-start | bytes 884740
  105.3 70.9 %all-to-all-start.5 = ((bf16[16,2,1,1,2,1152]{5,4,1,3,2,0:T(2,128)(2,1)}), bf16[16,2,1,1,2,1152]{5,4,1,3,2,0:T(2,128)(2,1)S(1)}, u32[]{:S(2)}, u32[]{:S(2)}) async-start(bf16[16,2,1,1,2,1152]{5,4,1,3,2,0:T(2,128)(2,1)} %copy.81), calls=%async_computation.5 | async-start | bytes 294912 | tf_op jit(solution)/shard_map/all_to_all | solution.py:37
Sparse Core Ops, SparseCore 0:
  10.1 74.3 all-gather.4
  86.6 77.0 all-gather.6
